TPU v7x, 32 devices: a whole 2x2x4 slice. The times are simulated.
32 devices in a mesh: row: 16 (over z, x, core), col: 2 (over y).
Axes of the slice: x: 2, y: 2, z: 4, core: 2. Of those that a mesh axis runs over, the one named last changes fastest.
Arguments:
- occupied_waves: bfloat16 [1024, 32768], P('row', 'col'), may hold values from -6 to 6
- virtual_waves: bfloat16 [512, 32768], P('row', 'col'), may hold values from -6 to 6
- occupied_decay: float32 [1024], replicated, may hold values from 0.02 to 1
- virtual_decay: float32 [512], replicated, may hold values from 0.02 to 1
Outputs:
- spectrum_real: float32 [512, 32, 1024], P('row', 'col')
- spectrum_imaginary: float32 [512, 32, 1024], P('row', 'col')
All inputs are finite; a program needn't handle non-finite values.
Results may differ from a plain program's by a relative error of at most 0.0041.
Values may be sent and summed in bfloat16 or wider, within the bound.
A program may use at most 128 MiB of HBM per device.

v0:
```python
import math
import jax
import jax.numpy as jnp
from jax import lax
from jax.sharding import PartitionSpec as P

NOCC = 1024
NVIR = 512
NA = 32
NB = 32
NC = 32
ROWS_DEV = 32
NGRID = 32768


def tables(length):
    index = jnp.arange(length, dtype=jnp.int32)
    phase = index[:, None] * index[None, :] % length
    angle = phase.astype(jnp.float32) * (2.0 * math.pi / length)
    return (jnp.cos(angle), jnp.sin(angle))


def apply_table(form, data, table):
    return jnp.einsum(form, data, table, precision=lax.Precision.HIGHEST)


def real_step(data, form, length):
    cosine, sine = tables(length)
    return (apply_table(form, data, cosine), -apply_table(form, data, sine))


def complex_step(real_part, imag_part, form, length):
    cosine, sine = tables(length)
    new_real = apply_table(form, real_part, cosine) + apply_table(form, imag_part, sine)
    new_imag = apply_table(form, imag_part, cosine) - apply_table(form, real_part, sine)
    return (new_real, new_imag)


def scale_rows(waves, decay):
    return (waves * decay[:, None]).astype(jnp.bfloat16)


def place(waves, window, start_col):
    block_cols = waves.shape[1]
    buffer = jnp.zeros((waves.shape[0], window + block_cols), jnp.bfloat16)
    buffer = lax.dynamic_update_slice(buffer, waves, (jnp.int32(0), start_col))
    return buffer[:, :window]


def on_device(occupied_waves, virtual_waves, occupied_decay, virtual_decay):
    block_cols = occupied_waves.shape[1]
    row_count = lax.axis_size("row")
    contract = (((0,), (0,)), ((), ()))
    factor = -1.0 / math.sqrt(NOCC * NVIR)
    window = ROWS_DEV * row_count
    start_col = lax.axis_index("col") * block_cols
    plane_cols = NB * NC
    per_col = block_cols // plane_cols
    spread = row_count // per_col
    sub_rows = ROWS_DEV // spread

    def spread_planes(waves):
        share = waves.shape[0]
        shaped = waves.reshape(share, per_col, 1, plane_cols)
        shaped = jnp.broadcast_to(shaped, (share, per_col, spread, plane_cols))
        return shaped.reshape(share, row_count * plane_cols)

    def pick_rows(waves):
        share = waves.shape[0]
        shaped = place(waves, window, start_col).reshape(share, row_count, spread, sub_rows)
        shaped = jnp.transpose(shaped, (0, 2, 1, 3))[:, None]
        shaped = jnp.broadcast_to(shaped, (share, per_col, spread, row_count, sub_rows))
        return shaped.reshape(share, row_count * row_count * sub_rows)

    plane_occ, plane_vir = (
        lax.all_to_all(
            spread_planes(occupied_waves), "row", split_axis=1, concat_axis=0, tiled=True
        ),
        lax.all_to_all(
            spread_planes(virtual_waves), "row", split_axis=1, concat_axis=0, tiled=True
        ),
    )
    part_occ, part_vir = (
        lax.all_to_all(pick_rows(occupied_waves), "row", split_axis=1, concat_axis=0, tiled=True),
        lax.all_to_all(pick_rows(virtual_waves), "row", split_axis=1, concat_axis=0, tiled=True),
    )
    occ_rows, vir_rows = (
        lax.psum(part_occ.astype(jnp.float32).astype(jnp.bfloat16), "col").astype(jnp.float32),
        lax.psum(part_vir.astype(jnp.float32).astype(jnp.bfloat16), "col").astype(jnp.float32),
    )
    occ_rows = scale_rows(occ_rows, occupied_decay)
    vir_rows = scale_rows(vir_rows, virtual_decay)
    green_occ = lax.dot_general(plane_occ, occ_rows, contract, preferred_element_type=jnp.float32)
    green_vir = lax.dot_general(plane_vir, vir_rows, contract, preferred_element_type=jnp.float32)
    polar = green_occ * green_vir * factor
    cube = polar.reshape(1, NB, NC, row_count * sub_rows)
    real_part, imag_part = real_step(cube, "abcr,cw->wabr", NC)
    real_part, imag_part = complex_step(real_part, imag_part, "wabr,bv->wavr", NB)
    blocked = (NC, 1, NB, row_count, sub_rows)
    real_part, imag_part = (
        lax.all_to_all(
            lax.all_to_all(
                real_part.reshape(blocked), "row", split_axis=3, concat_axis=3, tiled=True
            ),
            "col",
            split_axis=0,
            concat_axis=1,
            tiled=True,
        ),
        lax.all_to_all(
            lax.all_to_all(
                imag_part.reshape(blocked), "row", split_axis=3, concat_axis=3, tiled=True
            ),
            "col",
            split_axis=0,
            concat_axis=1,
            tiled=True,
        ),
    )

    def settle(part):
        kc_share = part.shape[0]
        part = part.reshape(kc_share, part.shape[1], NB, per_col, spread, sub_rows)
        part = jnp.transpose(part, (0, 1, 3, 2, 4, 5))
        return part.reshape(kc_share, NA, NB, ROWS_DEV)

    real_part, imag_part = complex_step(settle(real_part), settle(imag_part), "wavr,au->rwuv", NA)
    normal = 1.0 / math.sqrt(NGRID)
    final_shape = (real_part.shape[0], real_part.shape[1], NA * NB)
    return ((real_part * normal).reshape(final_shape), (imag_part * normal).reshape(final_shape))


def solution(mesh):
    in_specs = (P("row", "col"), P("row", "col"), P(), P())
    out_specs = (P("row", "col", None), P("row", "col", None))
    return jax.shard_map(
        on_device, mesh=mesh, in_specs=in_specs, out_specs=out_specs, check_vma=False
    )
```

profile of v0, /device:TPU:10, one launch (start us, length us, event | category | flops | bytes accessed | tf_op | source)
XLA Modules:
  0.0 507.3 jit_solution(10017124884010591523)
XLA Ops:
  9.4 6.2 %all-to-all-start.2 = ((bf16[32,16,512]{2,0,1:T(8,128)(2,1)}), bf16[32,16,512]{2,0,1:T(8,128)(2,1)S(1)}, u32[]{:S(2)}, u32[]{:S(2)}) async-start(bf16[32,16,512]{2,0,1:T(8,128)(2,1)} %broadcast_in_dim.11), calls=%async_computation.2 | async-start | bytes 1048576 | tf_op jit(solution)/shard_map/all_to_all | solution.py:85
  16.1 12.9 %all-to-all-done.2 = bf16[32,16,512]{2,0,1:T(8,128)(2,1)S(1)} async-done(((bf16[32,16,512]{2,0,1:T(8,128)(2,1)}), bf16[32,16,512]{2,0,1:T(8,128)(2,1)S(1)}, u32[]{:S(2)}, u32[]{:S(2)}) %all-to-all-start.2) | async-done | bytes 524320 | tf_op jit(solution)/shard_map/all_to_all | solution.py:85
  30.1 5.2 %all-to-all-start = ((bf16[64,16,512]{2,0,1:T(8,128)(2,1)}), bf16[64,16,512]{2,0,1:T(8,128)(2,1)S(1)}, u32[]{:S(2)}, u32[]{:S(2)}) async-start(bf16[64,16,512]{2,0,1:T(8,128)(2,1)} %broadcast_in_dim.9), calls=%async_computation | async-start | bytes 2097152 | tf_op jit(solution)/shard_map/all_to_all | solution.py:84
  36.8 23.0 %all-to-all-done = bf16[64,16,512]{2,0,1:T(8,128)(2,1)S(1)} async-done(((bf16[64,16,512]{2,0,1:T(8,128)(2,1)}), bf16[64,16,512]{2,0,1:T(8,128)(2,1)S(1)}, u32[]{:S(2)}, u32[]{:S(2)}) %all-to-all-start) | async-done | bytes 1048608 | tf_op jit(solution)/shard_map/all_to_all | solution.py:84
  60.8 5.2 %all-to-all-start.1 = ((bf16[64,16,1024]{2,0,1:T(8,128)(2,1)}), bf16[64,16,1024]{2,0,1:T(8,128)(2,1)S(1)}, u32[]{:S(2)}, u32[]{:S(2)}) async-start(bf16[64,16,1024]{2,0,1:T(8,128)(2,1)} %bitcast.123), calls=%async_computation.1 | async-start | bytes 4194304 | tf_op jit(solution)/shard_map/all_to_all | solution.py:76
  67.1 46.1 %all-to-all-done.1 = bf16[64,16,1024]{2,0,1:T(8,128)(2,1)S(1)} async-done(((bf16[64,16,1024]{2,0,1:T(8,128)(2,1)}), bf16[64,16,1024]{2,0,1:T(8,128)(2,1)S(1)}, u32[]{:S(2)}, u32[]{:S(2)}) %all-to-all-start.1) | async-done | bytes 2097184 | tf_op jit(solution)/shard_map/all_to_all | solution.py:76
  113.2 5.1 all-to-all-start.3
  119.0 55.5 %all-reduce.3.cloned.1.call-done = (bf16[1024,512]{1,0:T(8,128)(2,1)}, bf16[512,512]{1,0:T(8,128)(2,1)}) async-done(((bf16[1024,512]{1,0:T(8,128)(2,1)}, bf16[512,512]{1,0:T(8,128)(2,1)}), (bf16[1024,512]{1,0:T(8,128)(2,1)}, bf16[512,512]{1,0:T(8,128)(2,1)})) %all-reduce.3.cloned.1.call-update) | async-done | bytes 1572880 | tf_op jit(solution)/shard_map/psum | solution.py:88
  174.5 3.9 fusion.12
  178.5 3.9 multiply_bitcast_fusion.2
  187.7 4.3 fusion.29
  195.0 4.4 subtract_bitcast_fusion
  199.4 6.4 %reshape.86 = f32[32,1,32,16,32]{4,3,2,0,1:T(8,128)} reshape(f32[32,1,32,512]{3,2,0,1:T(8,128)} %subtract_bitcast_fusion) | data formatting | bytes 4194304 | tf_op jit(solution)/shard_map/reshape | solution.py:112
  205.8 9.3 %copy.71 = f32[32,1,32,16,32]{4,2,0,1,3:T(8,128)} copy(f32[32,1,32,16,32]{4,3,2,0,1:T(8,128)} %reshape.86) | data formatting | bytes 4194304 | tf_op jit(solution)/shard_map/reshape | solution.py:112
  215.1 8.6 %reshape.99 = f32[16,1,32768]{2,1,0:T(1,128)} reshape(f32[16,1,32,32,32]{4,3,2,1,0:T(8,128)} %bitcast.113) | data formatting | bytes 4194304
  223.7 6.1 %all-to-all-start.6 = ((f32[16,1,32768]{2,1,0:T(1,128)}), f32[16,1,32768]{2,1,0:T(1,128)}, u32[]{:S(2)}, u32[]{:S(2)}) async-start(f32[16,1,32768]{2,1,0:T(1,128)} %reshape.99), calls=%async_computation.6 | async-start | bytes 4194304 | tf_op jit(solution)/shard_map/all_to_all | solution.py:111
  229.7 4.6 fusion.2
  234.3 4.4 add_bitcast_fusion
  238.7 6.2 %reshape.83 = f32[32,1,32,16,32]{4,3,2,0,1:T(8,128)} reshape(f32[32,1,32,512]{3,2,0,1:T(8,128)} %add_bitcast_fusion) | data formatting | bytes 4194304 | tf_op jit(solution)/shard_map/reshape | solution.py:103
  244.9 9.3 %copy.72 = f32[32,1,32,16,32]{4,2,0,1,3:T(8,128)} copy(f32[32,1,32,16,32]{4,3,2,0,1:T(8,128)} %reshape.83) | data formatting | bytes 4194304 | tf_op jit(solution)/shard_map/reshape | solution.py:103
  254.2 8.6 %reshape.95 = f32[16,1,32768]{2,1,0:T(1,128)} reshape(f32[16,1,32,32,32]{4,3,2,1,0:T(8,128)} %bitcast.114) | data formatting | bytes 4194304
  262.7 14.2 %all-to-all-done.6 = f32[16,1,32768]{2,1,0:T(1,128)} async-done(((f32[16,1,32768]{2,1,0:T(1,128)}), f32[16,1,32768]{2,1,0:T(1,128)}, u32[]{:S(2)}, u32[]{:S(2)}) %all-to-all-start.6) | async-done | bytes 2097184 | tf_op jit(solution)/shard_map/all_to_all | solution.py:111
  277.0 5.6 %all-to-all-start.4 = ((f32[16,1,32768]{2,1,0:T(1,128)}), f32[16,1,32768]{2,1,0:T(1,128)}, u32[]{:S(2)}, u32[]{:S(2)}) async-start(f32[16,1,32768]{2,1,0:T(1,128)} %reshape.95), calls=%async_computation.4 | async-start | bytes 4194304 | tf_op jit(solution)/shard_map/all_to_all | solution.py:102
  283.2 7.3 %reduce.2 = f32[16,32768]{1,0:T(8,128)S(1)} reduce(f32[16,1,32768]{2,1,0:T(1,128)} %all-to-all-done.6, f32[]{:T(128)} %broadcast.102), dimensions={1}, to_apply=%all_to_all.98.reduce_sub_computation | reduce | bytes 4194308 | tf_op jit(solution)/shard_map/all_to_all | solution.py:111
  290.4 4.9 reshape.100
  295.4 14.2 %copy.45 = f32[32,1,32,16,32]{4,3,2,1,0:T(8,128)} copy(f32[32,1,32,16,32]{4,2,0,1,3:T(8,128)} %bitcast.115) | data formatting | bytes 4194304 | tf_op jit(solution)/shard_map/all_to_all | solution.py:111
  309.5 6.8 %reshape.101 = f32[2,1,262144]{2,1,0:T(1,128)} reshape(f32[32,1,32,16,32]{4,3,2,1,0:T(8,128)} %copy.45) | data formatting | bytes 4194304
  316.4 13.3 %all-to-all-done.4 = f32[16,1,32768]{2,1,0:T(1,128)} async-done(((f32[16,1,32768]{2,1,0:T(1,128)}), f32[16,1,32768]{2,1,0:T(1,128)}, u32[]{:S(2)}, u32[]{:S(2)}) %all-to-all-start.4) | async-done | bytes 2097184 | tf_op jit(solution)/shard_map/all_to_all | solution.py:102
  329.7 5.0 all-to-all-start.7
  334.7 7.3 %reduce = f32[16,32768]{1,0:T(8,128)S(1)} reduce(f32[16,1,32768]{2,1,0:T(1,128)} %all-to-all-done.4, f32[]{:T(128)} %broadcast.102), dimensions={1}, to_apply=%all_to_all.94.reduce_sub_computation | reduce | bytes 4194308 | tf_op jit(solution)/shard_map/all_to_all | solution.py:102
  342.0 4.8 reshape.96
  346.7 14.2 %copy.40 = f32[32,1,32,16,32]{4,3,2,1,0:T(8,128)} copy(f32[32,1,32,16,32]{4,2,0,1,3:T(8,128)} %bitcast.116) | data formatting | bytes 4194304 | tf_op jit(solution)/shard_map/all_to_all | solution.py:102
  360.9 6.8 %reshape.97 = f32[2,1,262144]{2,1,0:T(1,128)} reshape(f32[32,1,32,16,32]{4,3,2,1,0:T(8,128)} %copy.40) | data formatting | bytes 4194304
  367.8 4.8 all-to-all-start.5
  372.6 8.5 %reduce.3 = f32[2,262144]{1,0:T(2,128)S(1)} reduce(f32[2,1,262144]{2,1,0:T(1,128)} %all-to-all-done.7, f32[]{:T(128)} %broadcast.102), dimensions={1}, to_apply=%all_to_all.99.reduce_sub_computation | reduce | bytes 4194308 | tf_op jit(solution)/shard_map/all_to_all | solution.py:110
  381.1 6.4 %reshape.102 = f32[32,1,32,16,32]{4,3,2,1,0:T(8,128)} reshape(f32[2,262144]{1,0:T(2,128)S(1)} %reduce.3) | data formatting | bytes 4194304
  387.5 7.7 %copy.46 = f32[2,16,1,32,16,32]{5,4,0,3,1,2:T(8,128)} copy(f32[2,16,1,32,16,32]{5,4,3,1,0,2:T(8,128)} %bitcast.117) | data formatting | bytes 4194304 | tf_op jit(solution)/shard_map/all_to_all | solution.py:110
  398.3 8.2 %reduce.1 = f32[2,262144]{1,0:T(2,128)S(1)} reduce(f32[2,1,262144]{2,1,0:T(1,128)} %all-to-all-done.5, f32[]{:T(128)} %broadcast.102), dimensions={1}, to_apply=%all_to_all.95.reduce_sub_computation | reduce | bytes 4194308 | tf_op jit(solution)/shard_map/all_to_all | solution.py:101
  406.6 6.4 %reshape.98 = f32[32,1,32,16,32]{4,3,2,1,0:T(8,128)} reshape(f32[2,262144]{1,0:T(2,128)S(1)} %reduce.1) | data formatting | bytes 4194304
  413.0 4.6 copy.41
  417.6 9.5 %fusion.22 = f32[32,16,32,32]{3,0,2,1:T(8,128)} fusion(f32[16,32,32,32]{3,1,2,0:T(8,128)S(1)} %bitcast.111), kind=kOutput, calls=%fused_computation.31 | convolution fusion | flops 201340928 | bytes 4194304 | tf_op jit(solution)/shard_map/wavr,au->rwuv/dot_general | solution.py:24
  427.1 9.8 %fusion.20 = f32[32,16,32,32]{3,0,2,1:T(8,128)} fusion(f32[16,32,32,32]{3,1,2,0:T(8,128)S(1)} %bitcast.109), kind=kOutput, calls=%fused_computation.29 | convolution fusion | flops 201340928 | bytes 4194304 | tf_op jit(solution)/shard_map/wavr,au->rwuv/dot_general | solution.py:24
  436.9 12.1 %multiply_bitcast_fusion.1 = f32[32,16,32,32]{0,2,3,1:T(8,128)} fusion(f32[32,16,32,32]{3,0,2,1:T(8,128)} %fusion.22, f32[16,32,32,32]{3,1,2,0:T(8,128)S(1)} %bitcast.110), kind=kOutput, calls=%fused_computation.1 | convolution fusion | flops 202389504 | bytes 6291456 | tf_op jit(solution)/shard_map/wavr,au->rwuv/dot_general | solution.py:24
  449.0 12.4 %multiply_bitcast_fusion = f32[32,16,32,32]{0,2,3,1:T(8,128)} fusion(f32[32,16,32,32]{3,0,2,1:T(8,128)} %fusion.20, f32[16,32,32,32]{3,1,2,0:T(8,128)S(1)} %bitcast.112), kind=kOutput, calls=%fused_computation | convolution fusion | flops 202389504 | bytes 6291456 | tf_op jit(solution)/shard_map/wavr,au->rwuv/dot_general | solution.py:24
  461.4 11.7 %copy.48 = f32[32,16,32,32]{3,2,1,0:T(8,128)} copy(f32[32,16,32,32]{0,2,3,1:T(8,128)} %multiply_bitcast_fusion) | data formatting | bytes 4194304 | tf_op jit(solution)/shard_map/mul | solution.py:130
  473.1 7.7 %reshape.90 = f32[32,16,1024]{2,1,0:T(8,128)} reshape(f32[32,16,32,32]{3,2,1,0:T(8,128)} %copy.48) | data formatting | bytes 4194304 | tf_op jit(solution)/shard_map/reshape | solution.py:130
  480.8 11.7 %copy.47 = f32[32,16,32,32]{3,2,1,0:T(8,128)} copy(f32[32,16,32,32]{0,2,3,1:T(8,128)} %multiply_bitcast_fusion.1) | data formatting | bytes 4194304 | tf_op jit(solution)/shard_map/mul | solution.py:130
  492.5 7.7 %reshape.89 = f32[32,16,1024]{2,1,0:T(8,128)} reshape(f32[32,16,32,32]{3,2,1,0:T(8,128)} %copy.47) | data formatting | bytes 4194304 | tf_op jit(solution)/shard_map/reshape | solution.py:130
  (40 shorter events, 20.1 us)
Async XLA Ops:
  8.6 7.3 %copy-start.2 = (bf16[64,16384]{1,0:T(8,128)(2,1)S(1)}, bf16[64,16384]{1,0:T(8,128)(2,1)}, u32[]{:S(2)}) copy-start(bf16[64,16384]{1,0:T(8,128)(2,1)} %param.4) | copy-start | bytes 6291460
  9.4 19.5 %all-to-all-start.2 = ((bf16[32,16,512]{2,0,1:T(8,128)(2,1)}), bf16[32,16,512]{2,0,1:T(8,128)(2,1)S(1)}, u32[]{:S(2)}, u32[]{:S(2)}) async-start(bf16[32,16,512]{2,0,1:T(8,128)(2,1)} %broadcast_in_dim.11), calls=%async_computation.2 | async-start | bytes 1048576 | tf_op jit(solution)/shard_map/all_to_all | solution.py:85
  29.0 1.1 copy-start.5
  30.1 29.7 %all-to-all-start = ((bf16[64,16,512]{2,0,1:T(8,128)(2,1)}), bf16[64,16,512]{2,0,1:T(8,128)(2,1)S(1)}, u32[]{:S(2)}, u32[]{:S(2)}) async-start(bf16[64,16,512]{2,0,1:T(8,128)(2,1)} %broadcast_in_dim.9), calls=%async_computation | async-start | bytes 2097152 | tf_op jit(solution)/shard_map/all_to_all | solution.py:84
  59.9 1.0 copy-start.4
  60.8 5.2 %copy-start.3 = (bf16[32,16384]{1,0:T(8,128)(2,1)S(1)}, bf16[32,16384]{1,0:T(8,128)(2,1)}, u32[]{:S(2)}) copy-start(bf16[32,16384]{1,0:T(8,128)(2,1)} %param.5) | copy-start | bytes 3145732
  60.8 52.4 %all-to-all-start.1 = ((bf16[64,16,1024]{2,0,1:T(8,128)(2,1)}), bf16[64,16,1024]{2,0,1:T(8,128)(2,1)S(1)}, u32[]{:S(2)}, u32[]{:S(2)}) async-start(bf16[64,16,1024]{2,0,1:T(8,128)(2,1)} %bitcast.123), calls=%async_computation.1 | async-start | bytes 4194304 | tf_op jit(solution)/shard_map/all_to_all | solution.py:76
  67.1 107.4 %copy-start.6 = (f32[1024]{0:T(1024)S(1)}, f32[1024]{0:T(1024)}, u32[]{:S(2)}) copy-start(f32[1024]{0:T(1024)} %param.6) | copy-start | bytes 12292
  113.2 65.3 %all-to-all-start.3 = ((bf16[32,16,1024]{2,0,1:T(8,128)(2,1)}), bf16[32,16,1024]{2,0,1:T(8,128)(2,1)S(1)}, u32[]{:S(2)}, u32[]{:S(2)}) async-start(bf16[32,16,1024]{2,0,1:T(8,128)(2,1)} %bitcast.126), calls=%async_computation.3 | async-start | bytes 2097152 | tf_op jit(solution)/shard_map/all_to_all | solution.py:79
  118.3 56.3 %all-reduce.3.cloned.1.call-start = ((), (), s32[]{:S(2)}) async-start(), calls=%async_computation.8 | async-start | bytes 3145728 | tf_op jit(solution)/shard_map/psum | solution.py:88
  174.5 3.9 copy-start.7
  184.5 1.3 copy-start.1
  187.7 4.3 copy-start
  223.7 53.3 %all-to-all-start.6 = ((f32[16,1,32768]{2,1,0:T(1,128)}), f32[16,1,32768]{2,1,0:T(1,128)}, u32[]{:S(2)}, u32[]{:S(2)}) async-start(f32[16,1,32768]{2,1,0:T(1,128)} %reshape.99), calls=%async_computation.6 | async-start | bytes 4194304 | tf_op jit(solution)/shard_map/all_to_all | solution.py:111
  277.0 52.7 %all-to-all-start.4 = ((f32[16,1,32768]{2,1,0:T(1,128)}), f32[16,1,32768]{2,1,0:T(1,128)}, u32[]{:S(2)}, u32[]{:S(2)}) async-start(f32[16,1,32768]{2,1,0:T(1,128)} %reshape.95), calls=%async_computation.4 | async-start | bytes 4194304 | tf_op jit(solution)/shard_map/all_to_all | solution.py:102
  329.7 38.1 %all-to-all-start.7 = ((f32[2,1,262144]{2,1,0:T(1,128)}), f32[2,1,262144]{2,1,0:T(1,128)}, u32[]{:S(2)}, u32[]{:S(2)}) async-start(f32[2,1,262144]{2,1,0:T(1,128)} %reshape.101), calls=%async_computation.7 | async-start | bytes 4194304 | tf_op jit(solution)/shard_map/all_to_all | solution.py:110
  367.8 30.6 %all-to-all-start.5 = ((f32[2,1,262144]{2,1,0:T(1,128)}), f32[2,1,262144]{2,1,0:T(1,128)}, u32[]{:S(2)}, u32[]{:S(2)}) async-start(f32[2,1,262144]{2,1,0:T(1,128)} %reshape.97), calls=%async_computation.5 | async-start | bytes 4194304 | tf_op jit(solution)/shard_map/all_to_all | solution.py:101
  413.0 14.1 %slice-start = ((s8[8388608]{0:T(1024)(128)(4,1)}), s8[4194304]{0:T(1024)(128)(4,1)S(1)}, s32[]{:S(2)}) async-start(s8[8388608]{0:T(1024)(128)(4,1)} %bitcast.107), calls=%async_computation.9 | async-start | bytes 8388608
  417.6 9.5 %slice-start.1 = ((s8[8388608]{0:T(1024)(128)(4,1)}), s8[4194304]{0:T(1024)(128)(4,1)S(1)}, s32[]{:S(2)}) async-start(s8[8388608]{0:T(1024)(128)(4,1)} %bitcast.107), calls=%async_computation.10 | async-start | bytes 8388608
Sparse Core Ops, SparseCore 0:
  122.0 52.4 all-reduce.2
where the time goes:
time: 513 us; the launch traced here: 507 us
  local copies, waits for them, and re-layouts  175 us (34%)
  waiting for transfers between devices  169 us (33%)
  matrix products  74.2 us (14%)
  starting transfers between devices  43.2 us (8%)
  other arithmetic  31.2 us (6%)
  between operations  14.5 us (3%)
    dot_general x10, matrix products, apply_table(): return jnp.einsum(form, data, table, precision=lax.Precision.HIGHEST)  66.3 us
    unnamed x28, local copies, waits for them, and re-layouts  55.6 us
    psum x1, waiting for transfers between devices, on_device(): lax.psum(part_occ.astype(jnp.float32).astype(jnp.bfloat16), 'col')  55.5 us
    all_to_all x1, waiting for transfers between devices, on_device(): lax.all_to_all(spread_planes(occupied_waves), 'row', split_axis=1, concat...  46.1 us
    all_to_all x1, waiting for transfers between devices, on_device(): lax.all_to_all(pick_rows(occupied_waves), 'row', split_axis=1, concat_axi...  23 us
    reshape x2, local copies, waits for them, and re-layouts, on_device(): imag_part.reshape(blocked)  15.7 us
    reshape x2, local copies, waits for them, and re-layouts, on_device(): real_part.reshape(blocked)  15.5 us
    all_to_all x2, local copies, waits for them, and re-layouts, on_device(): lax.all_to_all(real_part.reshape(blocked), 'row', split_axis=3, concat_ax...  14.8 us
  transfers between devices with their start and end apart: 9, of which 7 were waited for; matrix products, arithmetic and copies ran while one was open for 26% of the time, Pallas kernels for 0%

commit v1 on v0

--- a/solution.py
+++ b/solution.py
@@ -11,6 +11,28 @@
 NC = 32
 ROWS_DEV = 32
 NGRID = 32768
+
+
+def in_blocks(x, dim, peers):
+    before, after = (x.shape[:dim], x.shape[dim + 1 :])
+    return jnp.moveaxis(x.reshape(*before, peers, -1, *after), dim, 0)
+
+
+def laid_out(pieces, dim):
+    dims = list(pieces.shape[1:])
+    dims[dim] *= pieces.shape[0]
+    return jnp.moveaxis(pieces, 0, dim).reshape(dims)
+
+
+def swapped_with_each(x, axis, split_dim, concat_dim):
+    size, place = (lax.axis_size(axis), lax.axis_index(axis))
+    blocks = in_blocks(x, split_dim, size)
+    finished = [blocks[place]]
+    for step in range(1, size):
+        sent = blocks[place ^ step]
+        finished.append(lax.ppermute(sent, axis, [(i, i ^ step) for i in range(size)]))
+    blocks = jnp.stack(finished)[place ^ jnp.arange(size)]
+    return laid_out(blocks, concat_dim)
 
 
 def tables(length):
@@ -73,9 +95,7 @@
         return shaped.reshape(share, row_count * row_count * sub_rows)
 
     plane_occ, plane_vir = (
-        lax.all_to_all(
-            spread_planes(occupied_waves), "row", split_axis=1, concat_axis=0, tiled=True
-        ),
+        swapped_with_each(spread_planes(occupied_waves), "row", 1, 0),
         lax.all_to_all(
             spread_planes(virtual_waves), "row", split_axis=1, concat_axis=0, tiled=True
         ),

time: 513 us -> 468 us (0.912)
  waiting for transfers between devices: 169 us -> 95.3 us
  local copies, waits for them, and re-layouts: 175 us -> 196 us
  starting transfers between devices: 43.2 us -> 55.3 us
  matrix products: 74.2 us -> 67.9 us
    ppermute x0 -> x15, waiting for transfers between devices: none -> 49 us  [swapped_with_each(): lax.ppermute(sent, axis, [(i, i ^ step) for i in range(size)])]
    psum x1, waiting for transfers between devices: 55.5 us -> 6.68 us  [on_device(): lax.psum(part_vir.astype(jnp.float32).astype(jnp.bfloat16), 'col')]
    all_to_all x1 -> x0, waiting for transfers between devices: 46.1 us -> none  [on_device(): lax.all_to_all(spread_planes(occupied_waves), 'row', split_axis=1, concat...]
    all_to_all x1, waiting for transfers between devices: 23 us -> 0.01 us  [on_device(): lax.all_to_all(pick_rows(occupied_waves), 'row', split_axis=1, concat_axi...]
    ppermute x0 -> x15, starting transfers between devices: none -> 15.8 us  [swapped_with_each(): lax.ppermute(sent, axis, [(i, i ^ step) for i in range(size)])]
    unnamed x28 -> x59, local copies, waits for them, and re-layouts: 55.6 us -> 71.1 us
    another operation x0 -> x2, local copies, waits for them, and re-layouts: none -> 6.73 us
    all_to_all x1 -> x0, starting transfers between devices: 5.24 us -> none  [on_device(): lax.all_to_all(spread_planes(occupied_waves), 'row', split_axis=1, concat...]
  transfers between devices with their start and end apart: 9 -> 23, of which waited for: 7 -> 15; matrix products, arithmetic and copies ran while one was open for 26% -> 32% of each run, Pallas kernels for 0% -> 0%
where the time goes in v1:
time: 468 us; the launch traced here: 460 us
  local copies, waits for them, and re-layouts  196 us (42%)
  waiting for transfers between devices  95.3 us (20%)
  matrix products  67.9 us (15%)
  starting transfers between devices  55.3 us (12%)
  other arithmetic  30.8 us (7%)
  between operations  15 us (3%)
    unnamed x59, local copies, waits for them, and re-layouts  71.1 us
    dot_general x10, matrix products, apply_table(): return jnp.einsum(form, data, table, precision=lax.Precision.HIGHEST)  64.6 us
    ppermute x15, waiting for transfers between devices, swapped_with_each(): lax.ppermute(sent, axis, [(i, i ^ step) for i in range(size)])  49 us
    ppermute x15, starting transfers between devices, swapped_with_each(): lax.ppermute(sent, axis, [(i, i ^ step) for i in range(size)])  15.8 us
    reshape x2, local copies, waits for them, and re-layouts, on_device(): imag_part.reshape(blocked)  15.5 us
    reshape x2, local copies, waits for them, and re-layouts, on_device(): real_part.reshape(blocked)  15.5 us
    all_to_all x2, local copies, waits for them, and re-layouts, on_device(): lax.all_to_all(real_part.reshape(blocked), 'row', split_axis=3, concat_ax...  14.7 us
    all_to_all x1, waiting for transfers between devices, on_device(): lax.all_to_all(imag_part.reshape(blocked), 'row', split_axis=3, concat_ax...  14.2 us
  transfers between devices with their start and end apart: 23, of which 15 were waited for; matrix products, arithmetic and copies ran while one was open for 32% of the time, Pallas kernels for 0%

profile of v1, /device:TPU:10, one launch (start us, length us, event | category | flops | bytes accessed | tf_op | source)
XLA Modules:
  0.0 460.1 jit_solution(5676458131485392163)
XLA Ops:
  9.4 6.2 %all-to-all-start.1 = ((bf16[32,16,512]{2,0,1:T(8,128)(2,1)}), bf16[32,16,512]{2,0,1:T(8,128)(2,1)S(1)}, u32[]{:S(2)}, u32[]{:S(2)}) async-start(bf16[32,16,512]{2,0,1:T(8,128)(2,1)} %broadcast_in_dim.11), calls=%async_computation.1 | async-start | bytes 1048576 | tf_op jit(solution)/shard_map/all_to_all | solution.py:105
  20.4 8.6 %all-to-all-done.1 = bf16[32,16,512]{2,0,1:T(8,128)(2,1)S(1)} async-done(((bf16[32,16,512]{2,0,1:T(8,128)(2,1)}), bf16[32,16,512]{2,0,1:T(8,128)(2,1)S(1)}, u32[]{:S(2)}, u32[]{:S(2)}) %all-to-all-start.1) | async-done | bytes 524320 | tf_op jit(solution)/shard_map/all_to_all | solution.py:105
  30.1 5.2 %all-to-all-start = ((bf16[64,16,512]{2,0,1:T(8,128)(2,1)}), bf16[64,16,512]{2,0,1:T(8,128)(2,1)S(1)}, u32[]{:S(2)}, u32[]{:S(2)}) async-start(bf16[64,16,512]{2,0,1:T(8,128)(2,1)} %broadcast_in_dim.9), calls=%async_computation | async-start | bytes 2097152 | tf_op jit(solution)/shard_map/all_to_all | solution.py:104
  35.3 6.1 %constant_dynamic-slice_fusion = (bf16[64,1,1024]{2,1,0:T(2,128)(2,1)S(1)}, bf16[64,1,1024]{2,1,0:T(2,128)(2,1)S(1)}, bf16[64,1,1024]{2,1,0:T(2,128)(2,1)S(1)}, ...) fusion(bf16[64,16,1024]{2,1,0:T(8,128)(2,1)S(1)} %bitcast.196, ...), kind=kLoop, calls=%fused_computation.88 | loop fusion | bytes 4194368 | tf_op jit(solution)/shard_map/dynamic-slice.15
  62.2 6.3 %collective-permute-done.5 = bf16[64,1024]{1,0:T(8,128)(2,1)S(1)} collective-permute-done((bf16[64,1024]{1,0:T(8,128)(2,1)S(1)}, bf16[64,1024]{1,0:T(8,128)(2,1)S(1)}, u32[]{:S(2)}, u32[]{:S(2)}) %collective-permute-start.5) | collective-permute-done | bytes 131104 | tf_op jit(solution)/shard_map/ppermute | solution.py:33
  71.0 6.3 %all-to-all-start.2 = ((bf16[32,16,1024]{2,0,1:T(8,128)(2,1)}), bf16[32,16,1024]{2,0,1:T(8,128)(2,1)S(1)}, u32[]{:S(2)}, u32[]{:S(2)}) async-start(bf16[32,16,1024]{2,0,1:T(8,128)(2,1)} %bitcast.166), calls=%async_computation.2 | async-start | bytes 2097152 | tf_op jit(solution)/shard_map/all_to_all | solution.py:99
  88.8 31.4 %collective-permute-done.11 = bf16[64,1024]{1,0:T(8,128)(2,1)S(1)} collective-permute-done((bf16[64,1024]{1,0:T(8,128)(2,1)S(1)}, bf16[64,1024]{1,0:T(8,128)(2,1)S(1)}, u32[]{:S(2)}, u32[]{:S(2)}) %collective-permute-start.11) | collective-permute-done | bytes 131104 | tf_op jit(solution)/shard_map/ppermute | solution.py:33
  122.4 3.3 collective-permute-done.13
  130.4 6.7 %all-reduce.3.cloned.1.call-done = (bf16[512,512]{1,0:T(8,128)(2,1)}, bf16[1024,512]{1,0:T(8,128)(2,1)}) async-done(((bf16[512,512]{1,0:T(8,128)(2,1)}, bf16[1024,512]{1,0:T(8,128)(2,1)}), (bf16[512,512]{1,0:T(8,128)(2,1)}, bf16[1024,512]{1,0:T(8,128)(2,1)})) %all-reduce.3.cloned.1.call-update) | async-done | bytes 1572880 | tf_op jit(solution)/shard_map/psum | solution.py:109
  144.4 3.0 fusion.1
  147.4 4.8 %subtract_bitcast_fusion = f32[32,1,32,512]{3,2,0,1:T(8,128)} fusion(f32[32,32,512]{2,0,1:T(8,128)S(1)} %fusion.1, f32[32,32,512]{2,0,1:T(8,128)S(1)} %fusion.30), kind=kOutput, calls=%fused_computation.5 | convolution fusion | flops 201865216 | bytes 6291456 | tf_op jit(solution)/shard_map/wabr,bv->wavr/dot_general | solution.py:46
  152.2 6.2 %reshape.134 = f32[32,1,32,16,32]{4,3,2,0,1:T(8,128)} reshape(f32[32,1,32,512]{3,2,0,1:T(8,128)} %subtract_bitcast_fusion) | data formatting | bytes 4194304 | tf_op jit(solution)/shard_map/reshape | solution.py:132
  158.4 9.3 %copy.114 = f32[32,1,32,16,32]{4,2,0,1,3:T(8,128)} copy(f32[32,1,32,16,32]{4,3,2,0,1:T(8,128)} %reshape.134) | data formatting | bytes 4194304 | tf_op jit(solution)/shard_map/reshape | solution.py:132
  167.7 8.6 %reshape.155 = f32[16,1,32768]{2,1,0:T(1,128)} reshape(f32[16,1,32,32,32]{4,3,2,1,0:T(8,128)} %bitcast.190) | data formatting | bytes 4194304
  176.3 6.1 %all-to-all-start.5 = ((f32[16,1,32768]{2,1,0:T(1,128)}), f32[16,1,32768]{2,1,0:T(1,128)}, u32[]{:S(2)}, u32[]{:S(2)}) async-start(f32[16,1,32768]{2,1,0:T(1,128)} %reshape.155), calls=%async_computation.5 | async-start | bytes 4194304 | tf_op jit(solution)/shard_map/all_to_all | solution.py:131
  182.4 4.6 fusion.3
  186.9 4.4 add_bitcast_fusion
  191.3 6.2 %reshape.131 = f32[32,1,32,16,32]{4,3,2,0,1:T(8,128)} reshape(f32[32,1,32,512]{3,2,0,1:T(8,128)} %add_bitcast_fusion) | data formatting | bytes 4194304 | tf_op jit(solution)/shard_map/reshape | solution.py:123
  197.5 9.3 %copy.115 = f32[32,1,32,16,32]{4,2,0,1,3:T(8,128)} copy(f32[32,1,32,16,32]{4,3,2,0,1:T(8,128)} %reshape.131) | data formatting | bytes 4194304 | tf_op jit(solution)/shard_map/reshape | solution.py:123
  206.8 8.6 %reshape.151 = f32[16,1,32768]{2,1,0:T(1,128)} reshape(f32[16,1,32,32,32]{4,3,2,1,0:T(8,128)} %bitcast.191) | data formatting | bytes 4194304
  215.4 14.2 %all-to-all-done.5 = f32[16,1,32768]{2,1,0:T(1,128)} async-done(((f32[16,1,32768]{2,1,0:T(1,128)}), f32[16,1,32768]{2,1,0:T(1,128)}, u32[]{:S(2)}, u32[]{:S(2)}) %all-to-all-start.5) | async-done | bytes 2097184 | tf_op jit(solution)/shard_map/all_to_all | solution.py:131
  229.6 5.4 %all-to-all-start.3 = ((f32[16,1,32768]{2,1,0:T(1,128)}), f32[16,1,32768]{2,1,0:T(1,128)}, u32[]{:S(2)}, u32[]{:S(2)}) async-start(f32[16,1,32768]{2,1,0:T(1,128)} %reshape.151), calls=%async_computation.3 | async-start | bytes 4194304 | tf_op jit(solution)/shard_map/all_to_all | solution.py:122
  235.5 7.2 %reduce.2 = f32[16,32768]{1,0:T(8,128)S(1)} reduce(f32[16,1,32768]{2,1,0:T(1,128)} %all-to-all-done.5, f32[]{:T(128)} %broadcast.135), dimensions={1}, to_apply=%all_to_all.80.reduce_sub_computation | reduce | bytes 4194308 | tf_op jit(solution)/shard_map/all_to_all | solution.py:131
  242.7 5.0 %reshape.156 = f32[16,1,32,32,32]{4,3,2,1,0:T(8,128)} reshape(f32[16,32768]{1,0:T(8,128)S(1)} %reduce.2) | data formatting | bytes 4194304
  247.7 14.2 %copy.42 = f32[32,1,32,16,32]{4,3,2,1,0:T(8,128)} copy(f32[32,1,32,16,32]{4,2,0,1,3:T(8,128)} %bitcast.192) | data formatting | bytes 4194304 | tf_op jit(solution)/shard_map/all_to_all | solution.py:131
  261.9 6.8 %reshape.157 = f32[2,1,262144]{2,1,0:T(1,128)} reshape(f32[32,1,32,16,32]{4,3,2,1,0:T(8,128)} %copy.42) | data formatting | bytes 4194304
  268.7 13.4 %all-to-all-done.3 = f32[16,1,32768]{2,1,0:T(1,128)} async-done(((f32[16,1,32768]{2,1,0:T(1,128)}), f32[16,1,32768]{2,1,0:T(1,128)}, u32[]{:S(2)}, u32[]{:S(2)}) %all-to-all-start.3) | async-done | bytes 2097184 | tf_op jit(solution)/shard_map/all_to_all | solution.py:122
  282.1 5.2 %all-to-all-start.6 = ((f32[2,1,262144]{2,1,0:T(1,128)}), f32[2,1,262144]{2,1,0:T(1,128)}, u32[]{:S(2)}, u32[]{:S(2)}) async-start(f32[2,1,262144]{2,1,0:T(1,128)} %reshape.157), calls=%async_computation.6 | async-start | bytes 4194304 | tf_op jit(solution)/shard_map/all_to_all | solution.py:130
  287.3 7.2 %reduce = f32[16,32768]{1,0:T(8,128)S(1)} reduce(f32[16,1,32768]{2,1,0:T(1,128)} %all-to-all-done.3, f32[]{:T(128)} %broadcast.135), dimensions={1}, to_apply=%all_to_all.76.reduce_sub_computation | reduce | bytes 4194308 | tf_op jit(solution)/shard_map/all_to_all | solution.py:122
  294.5 4.8 %reshape.152 = f32[16,1,32,32,32]{4,3,2,1,0:T(8,128)} reshape(f32[16,32768]{1,0:T(8,128)S(1)} %reduce) | data formatting | bytes 4194304
  299.3 14.2 %copy.37 = f32[32,1,32,16,32]{4,3,2,1,0:T(8,128)} copy(f32[32,1,32,16,32]{4,2,0,1,3:T(8,128)} %bitcast.193) | data formatting | bytes 4194304 | tf_op jit(solution)/shard_map/all_to_all | solution.py:122
  313.5 6.8 %reshape.153 = f32[2,1,262144]{2,1,0:T(1,128)} reshape(f32[32,1,32,16,32]{4,3,2,1,0:T(8,128)} %copy.37) | data formatting | bytes 4194304
  320.3 4.8 %all-to-all-start.4 = ((f32[2,1,262144]{2,1,0:T(1,128)}), f32[2,1,262144]{2,1,0:T(1,128)}, u32[]{:S(2)}, u32[]{:S(2)}) async-start(f32[2,1,262144]{2,1,0:T(1,128)} %reshape.153), calls=%async_computation.4 | async-start | bytes 4194304 | tf_op jit(solution)/shard_map/all_to_all | solution.py:121
  325.2 8.2 %reduce.3 = f32[2,262144]{1,0:T(2,128)S(1)} reduce(f32[2,1,262144]{2,1,0:T(1,128)} %all-to-all-done.6, f32[]{:T(128)} %broadcast.135), dimensions={1}, to_apply=%all_to_all.81.reduce_sub_computation | reduce | bytes 4194308 | tf_op jit(solution)/shard_map/all_to_all | solution.py:130
  333.3 6.4 %reshape.158 = f32[32,1,32,16,32]{4,3,2,1,0:T(8,128)} reshape(f32[2,262144]{1,0:T(2,128)S(1)} %reduce.3) | data formatting | bytes 4194304
  339.8 7.8 %copy.43 = f32[2,16,1,32,16,32]{5,4,0,3,1,2:T(8,128)} copy(f32[2,16,1,32,16,32]{5,4,3,1,0,2:T(8,128)} %bitcast.194) | data formatting | bytes 4194304 | tf_op jit(solution)/shard_map/all_to_all | solution.py:130
  347.5 3.4 all-to-all-done.4
  350.9 8.2 %reduce.1 = f32[2,262144]{1,0:T(2,128)S(1)} reduce(f32[2,1,262144]{2,1,0:T(1,128)} %all-to-all-done.4, f32[]{:T(128)} %broadcast.135), dimensions={1}, to_apply=%all_to_all.77.reduce_sub_computation | reduce | bytes 4194308 | tf_op jit(solution)/shard_map/all_to_all | solution.py:121
  359.1 6.4 %reshape.154 = f32[32,1,32,16,32]{4,3,2,1,0:T(8,128)} reshape(f32[2,262144]{1,0:T(2,128)S(1)} %reduce.1) | data formatting | bytes 4194304
  365.6 4.6 copy.38
  370.2 9.5 %fusion.23 = f32[32,16,32,32]{3,0,2,1:T(8,128)} fusion(f32[16,32,32,32]{3,1,2,0:T(8,128)S(1)} %bitcast.188), kind=kOutput, calls=%fused_computation.63 | convolution fusion | flops 201340928 | bytes 4194304 | tf_op jit(solution)/shard_map/wavr,au->rwuv/dot_general | solution.py:46
  379.7 9.8 %fusion.21 = f32[32,16,32,32]{3,0,2,1:T(8,128)} fusion(f32[16,32,32,32]{3,1,2,0:T(8,128)S(1)} %bitcast.186), kind=kOutput, calls=%fused_computation.61 | convolution fusion | flops 201340928 | bytes 4194304 | tf_op jit(solution)/shard_map/wavr,au->rwuv/dot_general | solution.py:46
  389.5 12.1 %multiply_bitcast_fusion.1 = f32[32,16,32,32]{0,2,3,1:T(8,128)} fusion(f32[32,16,32,32]{3,0,2,1:T(8,128)} %fusion.23, f32[16,32,32,32]{3,1,2,0:T(8,128)S(1)} %bitcast.187), kind=kOutput, calls=%fused_computation.2 | convolution fusion | flops 202389504 | bytes 6291456 | tf_op jit(solution)/shard_map/wavr,au->rwuv/dot_general | solution.py:46
  401.6 12.5 %multiply_bitcast_fusion = f32[32,16,32,32]{0,2,3,1:T(8,128)} fusion(f32[32,16,32,32]{3,0,2,1:T(8,128)} %fusion.21, f32[16,32,32,32]{3,1,2,0:T(8,128)S(1)} %bitcast.189), kind=kOutput, calls=%fused_computation.1 | convolution fusion | flops 202389504 | bytes 6291456 | tf_op jit(solution)/shard_map/wavr,au->rwuv/dot_general | solution.py:46
  414.1 11.6 %copy.45 = f32[32,16,32,32]{3,2,1,0:T(8,128)} copy(f32[32,16,32,32]{0,2,3,1:T(8,128)} %multiply_bitcast_fusion) | data formatting | bytes 4194304 | tf_op jit(solution)/shard_map/mul | solution.py:150
  425.8 7.7 %reshape.138 = f32[32,16,1024]{2,1,0:T(8,128)} reshape(f32[32,16,32,32]{3,2,1,0:T(8,128)} %copy.45) | data formatting | bytes 4194304 | tf_op jit(solution)/shard_map/reshape | solution.py:150
  433.5 11.6 %copy.44 = f32[32,16,32,32]{3,2,1,0:T(8,128)} copy(f32[32,16,32,32]{0,2,3,1:T(8,128)} %multiply_bitcast_fusion.1) | data formatting | bytes 4194304 | tf_op jit(solution)/shard_map/mul | solution.py:150
  445.1 7.7 %reshape.137 = f32[32,16,1024]{2,1,0:T(8,128)} reshape(f32[32,16,32,32]{3,2,1,0:T(8,128)} %copy.44) | data formatting | bytes 4194304 | tf_op jit(solution)/shard_map/reshape | solution.py:150
  (102 shorter events, 57.2 us)
Async XLA Ops:
  9.4 19.5 %all-to-all-start.1 = ((bf16[32,16,512]{2,0,1:T(8,128)(2,1)}), bf16[32,16,512]{2,0,1:T(8,128)(2,1)S(1)}, u32[]{:S(2)}, u32[]{:S(2)}) async-start(bf16[32,16,512]{2,0,1:T(8,128)(2,1)} %broadcast_in_dim.11), calls=%async_computation.1 | async-start | bytes 1048576 | tf_op jit(solution)/shard_map/all_to_all | solution.py:105
  18.5 1.6 copy-start.1
  29.0 1.2 copy-start.4
  30.1 40.9 %all-to-all-start = ((bf16[64,16,512]{2,0,1:T(8,128)(2,1)}), bf16[64,16,512]{2,0,1:T(8,128)(2,1)S(1)}, u32[]{:S(2)}, u32[]{:S(2)}) async-start(bf16[64,16,512]{2,0,1:T(8,128)(2,1)} %broadcast_in_dim.9), calls=%async_computation | async-start | bytes 2097152 | tf_op jit(solution)/shard_map/all_to_all | solution.py:104
  41.4 4.9 %copy-start.2 = (bf16[32,16384]{1,0:T(8,128)(2,1)S(1)}, bf16[32,16384]{1,0:T(8,128)(2,1)}, u32[]{:S(2)}) copy-start(bf16[32,16384]{1,0:T(8,128)(2,1)} %param.5) | copy-start | bytes 3145732
  41.4 6.4 %collective-permute-start = (bf16[64,1024]{1,0:T(8,128)(2,1)S(1)}, bf16[64,1024]{1,0:T(8,128)(2,1)S(1)}, u32[]{:S(2)}, u32[]{:S(2)}) collective-permute-start(bf16[64,1024]{1,0:T(8,128)(2,1)S(1)} %bitcast.219), channel_id=1, source_target_pairs={{0,2},{2,0},{4,6},{6,4},{8,10},{10,8},{12,14},{14,12},{16,18},{18,... | collective-permute-start | bytes 393224 | tf_op jit(solution)/shard_map/ppermute | solution.py:33
  41.6 7.9 %collective-permute-start.1 = (bf16[64,1024]{1,0:T(8,128)(2,1)S(1)}, bf16[64,1024]{1,0:T(8,128)(2,1)S(1)}, u32[]{:S(2)}, u32[]{:S(2)}) collective-permute-start(bf16[64,1024]{1,0:T(8,128)(2,1)S(1)} %bitcast.217), channel_id=1, source_target_pairs={{0,4},{2,6},{4,0},{6,2},{8,12},{10,14},{12,8},{14,10},{16,20},{18,... | collective-permute-start | bytes 393224 | tf_op jit(solution)/shard_map/ppermute | solution.py:33
  42.3 11.6 %collective-permute-start.2 = (bf16[64,1024]{1,0:T(8,128)(2,1)S(1)}, bf16[64,1024]{1,0:T(8,128)(2,1)S(1)}, u32[]{:S(2)}, u32[]{:S(2)}) collective-permute-start(bf16[64,1024]{1,0:T(8,128)(2,1)S(1)} %bitcast.216), channel_id=1, source_target_pairs={{0,6},{2,4},{4,2},{6,0},{8,14},{10,12},{12,10},{14,8},{16,22},{18,... | collective-permute-start | bytes 393224 | tf_op jit(solution)/shard_map/ppermute | solution.py:33
  43.6 13.7 %collective-permute-start.3 = (bf16[64,1024]{1,0:T(8,128)(2,1)S(1)}, bf16[64,1024]{1,0:T(8,128)(2,1)S(1)}, u32[]{:S(2)}, u32[]{:S(2)}) collective-permute-start(bf16[64,1024]{1,0:T(8,128)(2,1)S(1)} %bitcast.215), channel_id=1, source_target_pairs={{0,8},{2,10},{4,12},{6,14},{8,0},{10,2},{12,4},{14,6},{16,24},{18,... | collective-permute-start | bytes 393224 | tf_op jit(solution)/shard_map/ppermute | solution.py:33
  44.3 14.8 %collective-permute-start.4 = (bf16[64,1024]{1,0:T(8,128)(2,1)S(1)}, bf16[64,1024]{1,0:T(8,128)(2,1)S(1)}, u32[]{:S(2)}, u32[]{:S(2)}) collective-permute-start(bf16[64,1024]{1,0:T(8,128)(2,1)S(1)} %bitcast.214), channel_id=1, source_target_pairs={{0,10},{2,8},{4,14},{6,12},{8,2},{10,0},{12,6},{14,4},{16,26},{18,... | collective-permute-start | bytes 393224 | tf_op jit(solution)/shard_map/ppermute | solution.py:33
  47.8 20.7 %collective-permute-start.5 = (bf16[64,1024]{1,0:T(8,128)(2,1)S(1)}, bf16[64,1024]{1,0:T(8,128)(2,1)S(1)}, u32[]{:S(2)}, u32[]{:S(2)}) collective-permute-start(bf16[64,1024]{1,0:T(8,128)(2,1)S(1)} %bitcast.218), channel_id=1, source_target_pairs={{0,12},{2,14},{4,8},{6,10},{8,4},{10,6},{12,0},{14,2},{16,28},{18,... | collective-permute-start | bytes 393224 | tf_op jit(solution)/shard_map/ppermute | solution.py:33
  49.6 28.1 %collective-permute-start.6 = (bf16[64,1024]{1,0:T(8,128)(2,1)S(1)}, bf16[64,1024]{1,0:T(8,128)(2,1)}, u32[]{:S(2)}, u32[]{:S(2)}) collective-permute-start(bf16[64,1024]{1,0:T(8,128)(2,1)S(1)} %bitcast.213), channel_id=1, source_target_pairs={{0,14},{2,12},{4,10},{6,8},{8,6},{10,4},{12,2},{14,0},{16,30},{18,... | collective-permute-start | bytes 393224 | tf_op jit(solution)/shard_map/ppermute | solution.py:33
  53.9 26.9 %collective-permute-start.7 = (bf16[64,1024]{1,0:T(8,128)(2,1)S(1)}, bf16[64,1024]{1,0:T(8,128)(2,1)}, u32[]{:S(2)}, u32[]{:S(2)}) collective-permute-start(bf16[64,1024]{1,0:T(8,128)(2,1)S(1)} %bitcast.212), channel_id=1, source_target_pairs={{0,16},{2,18},{4,20},{6,22},{8,24},{10,26},{12,28},{14,30},{16,0},... | collective-permute-start | bytes 393224 | tf_op jit(solution)/shard_map/ppermute | solution.py:33
  57.3 25.0 %collective-permute-start.8 = (bf16[64,1024]{1,0:T(8,128)(2,1)S(1)}, bf16[64,1024]{1,0:T(8,128)(2,1)S(1)}, u32[]{:S(2)}, u32[]{:S(2)}) collective-permute-start(bf16[64,1024]{1,0:T(8,128)(2,1)S(1)} %bitcast.211), channel_id=1, source_target_pairs={{0,18},{2,16},{4,22},{6,20},{8,26},{10,24},{12,30},{14,28},{16,2},... | collective-permute-start | bytes 393224 | tf_op jit(solution)/shard_map/ppermute | solution.py:33
  59.1 25.5 %collective-permute-start.9 = (bf16[64,1024]{1,0:T(8,128)(2,1)S(1)}, bf16[64,1024]{1,0:T(8,128)(2,1)S(1)}, u32[]{:S(2)}, u32[]{:S(2)}) collective-permute-start(bf16[64,1024]{1,0:T(8,128)(2,1)S(1)} %bitcast.210), channel_id=1, source_target_pairs={{0,20},{2,22},{4,16},{6,18},{8,28},{10,30},{12,24},{14,26},{16,4},... | collective-permute-start | bytes 393224 | tf_op jit(solution)/shard_map/ppermute | solution.py:33
  68.5 18.7 %collective-permute-start.10 = (bf16[64,1024]{1,0:T(8,128)(2,1)S(1)}, bf16[64,1024]{1,0:T(8,128)(2,1)}, u32[]{:S(2)}, u32[]{:S(2)}) collective-permute-start(bf16[64,1024]{1,0:T(8,128)(2,1)S(1)} %bitcast.209), channel_id=1, source_target_pairs={{0,22},{2,20},{4,18},{6,16},{8,30},{10,28},{12,26},{14,24},{16,6},... | collective-permute-start | bytes 393224 | tf_op jit(solution)/shard_map/ppermute | solution.py:33
  71.0 11.3 %copy-start.3 = (bf16[64,16,512]{2,0,1:T(8,128)(2,1)}, bf16[64,16,512]{2,0,1:T(8,128)(2,1)S(1)}, u32[]{:S(2)}) copy-start(bf16[64,16,512]{2,0,1:T(8,128)(2,1)S(1)} %all-to-all-done) | copy-start | bytes 3145732
  71.0 59.4 %all-to-all-start.2 = ((bf16[32,16,1024]{2,0,1:T(8,128)(2,1)}), bf16[32,16,1024]{2,0,1:T(8,128)(2,1)S(1)}, u32[]{:S(2)}, u32[]{:S(2)}) async-start(bf16[32,16,1024]{2,0,1:T(8,128)(2,1)} %bitcast.166), calls=%async_computation.2 | async-start | bytes 2097152 | tf_op jit(solution)/shard_map/all_to_all | solution.py:99
  77.4 59.7 %all-reduce.3.cloned.1.call-start = ((), (), s32[]{:S(2)}) async-start(), calls=%async_computation.7 | async-start | bytes 3145728 | tf_op jit(solution)/shard_map/psum | solution.py:109
  77.7 42.6 %collective-permute-start.11 = (bf16[64,1024]{1,0:T(8,128)(2,1)S(1)}, bf16[64,1024]{1,0:T(8,128)(2,1)S(1)}, u32[]{:S(2)}, u32[]{:S(2)}) collective-permute-start(bf16[64,1024]{1,0:T(8,128)(2,1)S(1)} %bitcast.208), channel_id=1, source_target_pairs={{0,24},{2,26},{4,28},{6,30},{8,16},{10,18},{12,20},{14,22},{16,8},... | collective-permute-start | bytes 393224 | tf_op jit(solution)/shard_map/ppermute | solution.py:33
  80.8 41.0 %collective-permute-start.12 = (bf16[64,1024]{1,0:T(8,128)(2,1)S(1)}, bf16[64,1024]{1,0:T(8,128)(2,1)S(1)}, u32[]{:S(2)}, u32[]{:S(2)}) collective-permute-start(bf16[64,1024]{1,0:T(8,128)(2,1)S(1)} %bitcast.207), channel_id=1, source_target_pairs={{0,26},{2,24},{4,30},{6,28},{8,18},{10,16},{12,22},{14,20},{16,10}... | collective-permute-start | bytes 393224 | tf_op jit(solution)/shard_map/ppermute | solution.py:33
  82.4 43.4 %collective-permute-start.13 = (bf16[64,1024]{1,0:T(8,128)(2,1)S(1)}, bf16[64,1024]{1,0:T(8,128)(2,1)S(1)}, u32[]{:S(2)}, u32[]{:S(2)}) collective-permute-start(bf16[64,1024]{1,0:T(8,128)(2,1)S(1)} %bitcast.206), channel_id=1, source_target_pairs={{0,28},{2,30},{4,24},{6,26},{8,20},{10,22},{12,16},{14,18},{16,12}... | collective-permute-start | bytes 393224 | tf_op jit(solution)/shard_map/ppermute | solution.py:33
  84.6 42.9 %collective-permute-start.14 = (bf16[64,1024]{1,0:T(8,128)(2,1)S(1)}, bf16[64,1024]{1,0:T(8,128)(2,1)S(1)}, u32[]{:S(2)}, u32[]{:S(2)}) collective-permute-start(bf16[64,1024]{1,0:T(8,128)(2,1)S(1)} %bitcast.205), channel_id=1, source_target_pairs={{0,30},{2,28},{4,26},{6,24},{8,22},{10,20},{12,18},{14,16},{16,14}... | collective-permute-start | bytes 393224 | tf_op jit(solution)/shard_map/ppermute | solution.py:33
  128.1 9.0 %copy-start.5 = (f32[512]{0:T(512)S(1)}, f32[512]{0:T(512)}, u32[]{:S(2)}) copy-start(f32[512]{0:T(512)} %param.7) | copy-start | bytes 6148
  130.4 8.7 %copy-start.7 = (f32[1024]{0:T(1024)S(1)}, f32[1024]{0:T(1024)}, u32[]{:S(2)}) copy-start(f32[1024]{0:T(1024)} %param.6) | copy-start | bytes 12292
  137.1 2.0 copy-start.6
  142.4 2.0 copy-start
  176.3 53.3 %all-to-all-start.5 = ((f32[16,1,32768]{2,1,0:T(1,128)}), f32[16,1,32768]{2,1,0:T(1,128)}, u32[]{:S(2)}, u32[]{:S(2)}) async-start(f32[16,1,32768]{2,1,0:T(1,128)} %reshape.155), calls=%async_computation.5 | async-start | bytes 4194304 | tf_op jit(solution)/shard_map/all_to_all | solution.py:131
  229.6 52.5 %all-to-all-start.3 = ((f32[16,1,32768]{2,1,0:T(1,128)}), f32[16,1,32768]{2,1,0:T(1,128)}, u32[]{:S(2)}, u32[]{:S(2)}) async-start(f32[16,1,32768]{2,1,0:T(1,128)} %reshape.151), calls=%async_computation.3 | async-start | bytes 4194304 | tf_op jit(solution)/shard_map/all_to_all | solution.py:122
  282.1 38.3 %all-to-all-start.6 = ((f32[2,1,262144]{2,1,0:T(1,128)}), f32[2,1,262144]{2,1,0:T(1,128)}, u32[]{:S(2)}, u32[]{:S(2)}) async-start(f32[2,1,262144]{2,1,0:T(1,128)} %reshape.157), calls=%async_computation.6 | async-start | bytes 4194304 | tf_op jit(solution)/shard_map/all_to_all | solution.py:130
  320.3 30.6 %all-to-all-start.4 = ((f32[2,1,262144]{2,1,0:T(1,128)}), f32[2,1,262144]{2,1,0:T(1,128)}, u32[]{:S(2)}, u32[]{:S(2)}) async-start(f32[2,1,262144]{2,1,0:T(1,128)} %reshape.153), calls=%async_computation.4 | async-start | bytes 4194304 | tf_op jit(solution)/shard_map/all_to_all | solution.py:121
  365.6 14.1 %slice-start = ((s8[8388608]{0:T(1024)(128)(4,1)}), s8[4194304]{0:T(1024)(128)(4,1)S(1)}, s32[]{:S(2)}) async-start(s8[8388608]{0:T(1024)(128)(4,1)} %bitcast.184), calls=%async_computation.8 | async-start | bytes 8388608
  370.1 9.5 %slice-start.1 = ((s8[8388608]{0:T(1024)(128)(4,1)}), s8[4194304]{0:T(1024)(128)(4,1)S(1)}, s32[]{:S(2)}) async-start(s8[8388608]{0:T(1024)(128)(4,1)} %bitcast.184), calls=%async_computation.9 | async-start | bytes 8388608
Sparse Core Ops, SparseCore 0:
  82.5 54.5 all-reduce.2
